TPU v7x, 128 devices: a whole 4x4x4 slice. The times are simulated.
128 devices in a mesh: tau: 8 (over x, core), tile: 16 (over z, y).
Axes of the slice: x: 4, y: 4, z: 4, core: 2. Of those that a mesh axis runs over, the one named last changes fastest.
Arguments:
- occupied: bfloat16 [8, 2048, 128, 128], P('tau', 'tile'), may hold values from -6 to 6
- virtual: bfloat16 [8, 2048, 128, 128], P('tau', 'tile'), may hold values from -0.125 to 0.125
- cos_weights: float32 [4, 8], replicated, may hold values from -1 to 1
- pair_occ: int32 [3072, 16], P('tile'), may hold values from 0 to 127
- pair_virt: int32 [3072, 16], P('tile'), may hold values from 0 to 127
- partial_target_tile: int32 [3072], P('tile'), may hold values from 0 to 511, as said below
Outputs:
- spectrum: float32 [4, 512, 128, 128], P(None, 'tile', 'tau')
Inputs may be any that keep to these rules, and one draw needn't show every extreme that they name: `partial_target_tile`: within each aligned block of 192 entries, no owner (values d * 32 to (d + 1) * 32 - 1 for owner d) is named more than 24 times; one owner is named exactly 24 times in every block.
All inputs are finite; a program needn't handle non-finite values.
Results may differ from a plain program's by a relative error of at most 0.0003.
Values sent between devices are 32-bit elements; how exact they have to be, the bound alone decides.
No kernel may reach another device: no remote copies, remote signals or barrier semaphores. Data moves between devices by JAX's collectives and lax.ppermute only.
A program may use at most 192 MiB of HBM per device.

v0:
```python
import jax
import jax.numpy as jnp
from jax import lax
from jax.experimental import pallas as pl
from jax.experimental.pallas import tpu as pltpu
from jax.sharding import PartitionSpec as P


TILE = 128
SUB = 8
CHI_DEV = 32
STRIP = 16
TILE_FIRST = (48, 64)
TAU_FIRST = 80
SIDE = 4


def shifts(ntau):
    return [(s, h) for s in range(ntau // 2) for h in range(2)]


def partner(me, shift, ntau, back=False):
    s, h = shift
    chips = ntau // 2
    chip = (me // 2 + (chips - s if back else s)) % chips
    core = (me % 2 + h) % 2
    return 2 * chip + core


def product_of(occ_index, virt_index, occupied, virtual, p, terms):
    left = jnp.concatenate([occupied[occ_index[j, p]] for j in range(terms)], axis=1)
    right = jnp.concatenate([virtual[virt_index[j, p]] for j in range(terms)], axis=0)
    return jnp.dot(left, right, preferred_element_type=jnp.float32)


def load(pairs, arrived):
    copies = [pltpu.make_async_copy(a, b, arrived.at[i]) for i, (a, b) in enumerate(pairs)]
    for copy in copies:
        copy.start()
    for copy in copies:
        copy.wait()


def around(me, s, u, z_first, back=False):
    dz, dy = (s, u) if z_first else (u, s)
    z, y = me // SIDE, me % SIDE
    if back:
        return (z + SIDE - dz) % SIDE * SIDE + (y + SIDE - dy) % SIDE
    return (z + dz) % SIDE * SIDE + (y + dy) % SIDE


def tile_first_kernel(occ_index, virt_index, occ_far, virt_far, target, *refs, terms, spans):
    n = len(spans) * SIDE
    outs, halves, (occupied, virtual, arrived, left) = refs[:n], refs[n : n + len(spans)], refs[n + len(spans) :]
    load([(occ_far, occupied), (virt_far, virtual)], arrived)
    me = lax.axis_index("tile")
    copies = []
    for half, ((start, count), rows) in enumerate(zip(spans, halves)):
        strips, slots = rows.shape[:2]
        flat = rows.reshape(strips * slots * SUB, TILE)

        def step(g, carry, start=start, slots=slots, flat=flat):
            for q in range(SUB):
                p = g * SUB + q
                product = product_of(occ_index, virt_index, occupied, virtual, start + p, terms)
                for v in range(TILE // SUB):
                    i, h = divmod(v, 2)
                    at = (h * SUB * slots + p) * SUB + i
                    flat[pl.ds(at, SUB, stride=slots * SUB), :] = product[v * SUB : (v + 1) * SUB]
            return carry

        lax.fori_loop(0, count // SUB, step, 0)
        if half == 0:
            for b in range(strips):
                rows[b, count] = target[...]
        for s in range(SIDE):
            for u in range(SIDE):
                out = outs[half * SIDE + s]
                source = rows.at[around(me, s, u, half == 0), pl.ds(0, out.shape[1])]
                copies.append(pltpu.make_async_copy(source, out.at[u], left.at[len(copies)]))
                copies[-1].start()
    for copy in copies:
        copy.wait()


def tile_first_products(occ_index, virt_index, occupied, virtual, target, spans, terms, strips):
    far = pl.BlockSpec(memory_space=pltpu.HBM)
    store = pltpu.VMEM(occupied.shape, occupied.dtype)

    def kernel(*refs):
        tile_first_kernel(*refs, terms=terms, spans=spans)

    sizes = [count + (half == 0) for half, (_, count) in enumerate(spans)]
    return pl.pallas_call(
        kernel,
        out_shape=[jax.ShapeDtypeStruct((SIDE, n, SUB, TILE), jnp.float32) for n in sizes for _ in range(SIDE)],
        grid_spec=pltpu.PrefetchScalarGridSpec(
            num_scalar_prefetch=2,
            grid=(1,),
            in_specs=[far, far, pl.BlockSpec((SUB, TILE), lambda g, *_: (0, 0))],
            out_specs=[far] * (SIDE * len(spans)),
            scratch_shapes=[pltpu.VMEM((strips, count + 1, SUB, TILE), jnp.float32) for _, count in spans]
            + [store, store, pltpu.SemaphoreType.DMA((2,)), pltpu.SemaphoreType.DMA((strips * len(spans),))],
        ),
        compiler_params=pltpu.CompilerParams(vmem_limit_bytes=60 * 2**20),
        name="tile_first_products",
    )(occ_index, virt_index, occupied, virtual, target)


def tau_first_kernel(occ_index, virt_index, occ_far, virt_far, *refs, terms, start, count, ntau):
    outs, (strips, occupied, virtual, arrived, left) = refs[:ntau], refs[ntau:]
    load([(occ_far, occupied), (virt_far, virtual)], arrived)
    slots = strips.shape[2]
    flat = strips.reshape(ntau * STRIP * slots, TILE)

    def step(g, carry):
        for q in range(SUB):
            p = g * SUB + q
            product = product_of(occ_index, virt_index, occupied, virtual, start + p, terms)
            for v in range(TILE // SUB):
                flat[pl.ds(v * SUB * slots + p, SUB, stride=slots), :] = product[v * SUB : (v + 1) * SUB]
        return carry

    lax.fori_loop(0, count // SUB, step, 0)
    me = lax.axis_index("tau")
    copies = []
    for i, shift in enumerate(shifts(ntau)):
        source = strips.at[partner(me, shift, ntau), :, pl.ds(0, count)]
        copies.append(pltpu.make_async_copy(source, outs[i], left.at[i]))
    for copy in copies:
        copy.start()
    for copy in copies:
        copy.wait()


def tau_first_products(occ_index, virt_index, occupied, virtual, start, count, terms, ntau):
    far = pl.BlockSpec(memory_space=pltpu.HBM)
    store = pltpu.VMEM(occupied.shape, occupied.dtype)
    slots = count if count // SUB % 2 else count + SUB

    def kernel(*refs):
        tau_first_kernel(*refs, terms=terms, start=start, count=count, ntau=ntau)

    return pl.pallas_call(
        kernel,
        out_shape=[jax.ShapeDtypeStruct((STRIP, count, TILE), jnp.float32)] * ntau,
        grid_spec=pltpu.PrefetchScalarGridSpec(
            num_scalar_prefetch=2,
            grid=(1,),
            in_specs=[far, far],
            out_specs=[far] * ntau,
            scratch_shapes=[
                pltpu.VMEM((ntau, STRIP, slots, TILE), jnp.float32),
                store,
                store,
                pltpu.SemaphoreType.DMA((2,)),
                pltpu.SemaphoreType.DMA((ntau,)),
            ],
        ),
        compiler_params=pltpu.CompilerParams(vmem_limit_bytes=60 * 2**20),
        name="tau_first_products",
    )(occ_index, virt_index, occupied, virtual)


def weigh_kernel(weights, *refs, ntau, nfreq):
    *strips, out = refs
    me = lax.axis_index("tau")
    times = [partner(me, shift, ntau, back=True) for shift in shifts(ntau)]
    scale = [[jnp.full((SUB, TILE), weights[k * ntau + t], jnp.float32) for t in times] for k in range(nfreq)]

    def step(row, carry):
        for at in range(0, out.shape[2], SUB):
            values = [strip[row, at : at + SUB, :] for strip in strips]
            for k in range(nfreq):
                total = scale[k][0] * values[0]
                for t in range(1, ntau):
                    total = total + scale[k][t] * values[t]
                out[row, k, at : at + SUB, :] = total
        return carry

    lax.fori_loop(0, out.shape[0], step, 0)


def weigh(weights, strips, nfreq):
    ntau = len(strips)
    rows, count, width = strips[0].shape
    per = 4

    def kernel(*refs):
        weigh_kernel(*refs, ntau=ntau, nfreq=nfreq)

    return pl.pallas_call(
        kernel,
        out_shape=jax.ShapeDtypeStruct((rows, nfreq, count, width), jnp.float32),
        grid_spec=pltpu.PrefetchScalarGridSpec(
            num_scalar_prefetch=1,
            grid=(rows // per,),
            in_specs=[pl.BlockSpec((per, count, width), lambda g, *_: (g, 0, 0))] * ntau,
            out_specs=pl.BlockSpec((per, nfreq, count, width), lambda g, *_: (g, 0, 0, 0)),
        ),
        compiler_params=pltpu.CompilerParams(vmem_limit_bytes=60 * 2**20),
        name="weigh",
    )(weights, *strips)


def add_tile_first_kernel(target, *refs, spans, stride, ntau):
    *refs, turned = refs
    n = 2 * SIDE
    sums, outs = refs[-n:], refs[-n - ntau : -n]
    me = lax.axis_index("tau")
    order = [partner(me, shift, ntau) for shift in shifts(ntau)]
    for acc in sums:
        acc[...] = jnp.zeros_like(acc)
    work = []
    for half, (start, count) in enumerate(spans):
        near, far = refs[half * (2 * SIDE - 1) :][:SIDE], refs[half * (2 * SIDE - 1) + SIDE :][: SIDE - 1]
        for u in range(SIDE):
            rows = [far[u - 1].at[s] if u else near[s].at[0] for s in range(SIDE)]
            places = [(s, u) if half == 0 else (u, s) for s in range(SIDE)]
            bases = [(dz * SIDE + dy) * stride + start for dz, dy in places]

            work.append((rows, bases, count))
    for u in range(SIDE):
        first, second = work[u], work[u + SIDE]
        both = (first[0] + second[0], first[1] + second[1])
        middle, end = sorted((first[2] // SUB, second[2] // SUB))
        longer = max(first, second, key=lambda item: item[2])
        for (rows, bases), low, high in ((both, 0, middle), (longer[:2], middle, end)):

            def add(g, carry, rows=rows, bases=bases):
                for q in range(SUB):
                    p = g * SUB + q
                    for ref, base, acc in zip(rows, bases, sums):
                        acc[target[base + p]] += ref[p]
                return carry

            if low < high:
                lax.fori_loop(low, high, add, 0)

    def turn(g, carry):
        at = pl.multiple_of(g * SUB, SUB)
        total = sum([acc[pl.ds(at, SUB)] for acc in sums[1:]], sums[0][pl.ds(at, SUB)])
        turned[:, pl.ds(at, SUB), :] = jnp.swapaxes(total, 0, 1)
        return carry

    lax.fori_loop(0, sums[0].shape[0] // SUB, turn, 0)
    for r, out in zip(order, outs):
        out[...] = turned[r]


def add_tile_first(target, halves, spans, stride, ntau):
    tiles = SIDE * SIDE * CHI_DEV
    operands, specs = [], []
    for near, far in halves:
        operands += [*near, *far]
        specs += [pl.BlockSpec((1, *p.shape[1:]), lambda b, *_: (0, 0, 0, 0)) for p in near]
        specs += [pl.BlockSpec(p.shape, lambda b, *_: (0, 0, 0, 0)) for p in far]

    def kernel(*refs):
        add_tile_first_kernel(*refs, spans=spans, stride=stride, ntau=ntau)

    return pl.pallas_call(
        kernel,
        out_shape=[jax.ShapeDtypeStruct((tiles, TILE), jnp.float32)] * ntau,
        grid_spec=pltpu.PrefetchScalarGridSpec(
            num_scalar_prefetch=1,
            grid=(1,),
            in_specs=specs,
            out_specs=[pl.BlockSpec((tiles, TILE), lambda b, *_: (0, 0))] * ntau,
            scratch_shapes=[pltpu.VMEM((tiles, ntau, TILE), jnp.float32)] * (2 * SIDE)
            + [pltpu.VMEM((ntau, tiles, TILE), jnp.float32)],
        ),
        compiler_params=pltpu.CompilerParams(vmem_limit_bytes=60 * 2**20),
        name="add_tile_first",
    )(target, *operands)


def finish_kernel(target, weights, piece, *refs, start, stride, ntau, nfreq):
    times, out, sums = refs[:ntau], refs[ntau], refs[ntau + 1 :]
    step = pl.program_id(0)
    here = lax.axis_index("tau")
    origins = [partner(here, shift, ntau, back=True) for shift in shifts(ntau)]
    lower = lax.broadcasted_iota(jnp.int32, (SUB, TILE), 0) < nfreq
    me = lax.axis_index("tile")
    dz = (me // SIDE + SIDE - step) % SIDE
    bases = [(dz * SIDE + (me % SIDE + SIDE - y) % SIDE) * stride + start for y in range(SIDE)]

    @pl.when(step == 0)
    def _():
        for acc in sums:
            acc[...] = jnp.zeros_like(acc)

    def add(g, carry):
        at = pl.multiple_of(g * SUB, SUB)
        blocks = [piece[i, :, pl.ds(at, SUB), :] for i in range(SIDE)]
        pairs = [jnp.swapaxes(jnp.concatenate(blocks[i : i + 2], axis=0), 0, 1) for i in (0, 2)]
        for q in range(SUB):
            for i in range(SIDE):
                both = pairs[i // 2][q]
                mine = jnp.where(lower, 0.0, both) if i % 2 else jnp.where(lower, both, 0.0)
                sums[i][target[bases[i] + at + q]] += mine
        return carry

    lax.fori_loop(0, piece.shape[2] // SUB, add, 0)

    @pl.when(step == pl.num_programs(0) - 1)
    def _():
        scale = [[jnp.full((SUB, TILE), weights[k * ntau + t], jnp.float32) for t in origins] for k in range(nfreq)]

        def last(g, carry):
            at = pl.multiple_of(g * SUB, SUB)
            total = sum([acc[pl.ds(at, SUB)] for acc in sums[1:]], sums[0][pl.ds(at, SUB)])
            total = jnp.swapaxes(total, 0, 1)
            values = [part[pl.ds(at, SUB), :] for part in times]
            owner = g // (CHI_DEV // SUB)
            place = pl.multiple_of((g % (CHI_DEV // SUB)) * SUB, SUB)
            for k in range(nfreq):
                value = total[k] + total[k + nfreq]
                for factor, part in zip(scale[k], values):
                    value = value + factor * part
                out[owner, k, pl.ds(place, SUB), :] = value
            return carry

        lax.fori_loop(0, sums[0].shape[0] // SUB, last, 0)


def finish(target, weights, piece, start, times, stride, nfreq):
    ntau = len(times)
    tiles, width = times[0].shape
    blocks = tiles // CHI_DEV
    shape = (blocks, nfreq, CHI_DEV, width)

    def kernel(*refs):
        finish_kernel(*refs, start=start, stride=stride, ntau=ntau, nfreq=nfreq)

    return pl.pallas_call(
        kernel,
        out_shape=jax.ShapeDtypeStruct(shape, jnp.float32),
        grid_spec=pltpu.PrefetchScalarGridSpec(
            num_scalar_prefetch=2,
            grid=(blocks // SIDE,),
            in_specs=[pl.BlockSpec((SIDE, nfreq, piece.shape[2], width), lambda b, *_: (b, 0, 0, 0))]
            + [pl.BlockSpec((tiles, width), lambda b, *_: (0, 0))] * ntau,
            out_specs=pl.BlockSpec(shape, lambda b, *_: (0, 0, 0, 0)),
            scratch_shapes=[pltpu.VMEM((tiles, SUB, width), jnp.float32)] * SIDE,
        ),
        compiler_params=pltpu.CompilerParams(vmem_limit_bytes=50 * 2**20),
        name="finish",
    )(target, weights, piece, *times)


def turn_kernel(*refs):
    near, outs, held, arrived, left = refs[:SIDE], refs[SIDE:-3], *refs[-3:]
    inward = []
    for u in range(1, SIDE):
        for s in range(SIDE):
            at = (u - 1) * SIDE + s
            inward.append(pltpu.make_async_copy(near[s].at[u], held.at[u - 1, s], arrived.at[at]))
    outward = [pltpu.make_async_copy(held.at[u], out, left.at[u]) for u, out in enumerate(outs)]
    for copy in inward:
        copy.start()
    for u, copy in enumerate(outward):
        for s in range(SIDE):
            inward[u * SIDE + s].wait()
        copy.start()
    for copy in outward:
        copy.wait()


def turn(near):
    anywhere = pl.BlockSpec(memory_space=pltpu.HBM)
    return pl.pallas_call(
        turn_kernel,
        out_shape=[jax.ShapeDtypeStruct(near[0].shape, jnp.float32)] * (SIDE - 1),
        in_specs=[pl.BlockSpec(memory_space=pl.ANY)] * SIDE,
        out_specs=[anywhere] * (SIDE - 1),
        scratch_shapes=[
            pltpu.VMEM((SIDE - 1, *near[0].shape), jnp.float32),
            pltpu.SemaphoreType.DMA((SIDE * (SIDE - 1),)),
            pltpu.SemaphoreType.DMA((SIDE - 1,)),
        ],
        compiler_params=pltpu.CompilerParams(vmem_limit_bytes=60 * 2**20),
        name="turn",
    )(*near)


def over_tau(strips):
    ntau = len(strips)
    return [strips[0]] + [
        lax.ppermute(strip, "tau", [(i, partner(i, shift, ntau)) for i in range(ntau)])
        for strip, shift in zip(strips[1:], shifts(ntau)[1:])
    ]


def over_tile(rows, s, u, z_first):
    n = SIDE * SIDE
    return lax.ppermute(rows, "tile", [(i, around(i, s, u, z_first)) for i in range(n)])


def body(occupied, virtual, cos_weights, pair_occ, pair_virt, partial_target_tile):
    ntau = lax.axis_size("tau")
    blocks = lax.axis_size("tile")
    part, terms = pair_occ.shape
    nfreq = cos_weights.shape[0]
    weights = cos_weights.reshape(-1)
    occ_index = pair_occ.T
    virt_index = pair_virt.T
    slot = jnp.pad(partial_target_tile.astype(jnp.float32), (0, SUB * TILE - part)).reshape(SUB, TILE)
    stores = occupied[0], virtual[0]
    first, second = TILE_FIRST
    spans = [(0, first), (first, second)]

    near, far = [], []
    outs = list(tile_first_products(occ_index, virt_index, *stores, slot, spans, terms, blocks))
    occ_index, outs[0] = lax.optimization_barrier((occ_index, outs[0]))
    for half in range(2):
        mine, *others = outs[half * SIDE : (half + 1) * SIDE]
        near.append([mine] + [over_tile(rows, s + 1, 0, half == 0) for s, rows in enumerate(others)])
    strips = list(tau_first_products(occ_index, virt_index, *stores, first + second, TAU_FIRST, terms, ntau))
    strips = over_tau(strips)
    for half in range(2):
        far.append([over_tile(rows, 0, u + 1, half == 0) for u, rows in enumerate(turn(near[half]))])
    weighted = weigh(weights, strips, nfreq)
    piece = lax.all_to_all(weighted, "tile", 0, 0, tiled=True)

    lines = -(-part // TILE)
    stride = lines * TILE
    by_u = [jnp.stack([n[0, first, :lines] for n in near[0]])] + [f[:, first, :lines] for f in far[0]]
    target = jnp.stack(by_u, axis=1).astype(jnp.int32).reshape(-1)
    chi = add_tile_first(target, list(zip(near, far)), spans, stride, ntau)
    times = over_tau(chi)
    spectrum = finish(target, weights, piece, first + second, times, stride, nfreq)
    owned = lax.all_to_all(spectrum, "tile", 0, 0, tiled=True)
    return jnp.transpose(owned, (1, 2, 0, 3))


def solution(mesh):
    in_specs = (
        P("tau", "tile", None, None),
        P("tau", "tile", None, None),
        P(),
        P("tile", None),
        P("tile", None),
        P("tile"),
    )
    out_specs = P(None, "tile", "tau", None)

    return jax.shard_map(body, mesh=mesh, in_specs=in_specs, out_specs=out_specs, check_vma=False)
```

profile of v0, /device:TPU:0, one launch (start us, length us, event | category | flops | bytes accessed | tf_op | source)
XLA Modules:
  0.0 304.2 jit_solution(15949348187444485060)
XLA Ops:
  1.3 25.3 %tile_first_products.1 = (f32[4,49,8,128]{3,2,1,0:T(8,128)}, f32[4,49,8,128]{3,2,1,0:T(8,128)}, f32[4,49,8,128]{3,2,1,0:T(8,128)}, f32[4,49,8,128]{3,2,1,0:T(8,1...) custom-call(s32[16,192]{1,0:T(8,128)} %bitcast.25, ...), custom_call_target="tpu_custom_call" | custom-call | tf_op jit(solution)/shard_map/tile_first_products/pallas_call | solution.py:94
  26.6 19.8 %tau_first_products.1 = (f32[16,80,128]{2,1,0:T(8,128)}, f32[16,80,128]{2,1,0:T(8,128)}, f32[16,80,128]{2,1,0:T(8,128)}, f32[16,80,128]{2,1,0:T(8,128)}, f32[16,...) custom-call(s32[16,192]{1,0:T(8,128)} %bitcast.26, ...), custom_call_target="tpu_custom_call" | custom-call | tf_op jit(solution)/shard_map/tau_first_products/pallas_call | solution.py:144
  46.3 2.7 collective-permute-start.10
  49.0 1.1 collective-permute-start.11
  50.5 1.7 collective-permute-start.7
  52.3 12.8 %collective-permute-done.10.refs_6_ = f32[16,80,128]{2,1,0:T(8,128)S(1)} collective-permute-done((f32[16,80,128]{2,1,0:T(8,128)}, f32[16,80,128]{2,1,0:T(8,128)S(1)}, u32[]{:S(2)}, u32[]{:S(2)}) %collective-permute-start.10) | collective-permute-done | bytes 655392 | tf_op jit(solution)/shard_map/ppermute | solution.py:390
  65.1 0.8 copy-done.10
  65.9 2.2 collective-permute-start
  68.1 11.4 %collective-permute-done.11.refs_7_ = f32[16,80,128]{2,1,0:T(8,128)S(1)} collective-permute-done((f32[16,80,128]{2,1,0:T(8,128)}, f32[16,80,128]{2,1,0:T(8,128)S(1)}, u32[]{:S(2)}, u32[]{:S(2)}) %collective-permute-start.11) | collective-permute-done | bytes 655392 | tf_op jit(solution)/shard_map/ppermute | solution.py:390
  79.5 1.0 collective-permute-start.8
  80.5 13.0 %collective-permute-done.12.refs_8_ = f32[16,80,128]{2,1,0:T(8,128)S(1)} collective-permute-done((f32[16,80,128]{2,1,0:T(8,128)}, f32[16,80,128]{2,1,0:T(8,128)S(1)}, u32[]{:S(2)}, u32[]{:S(2)}) %collective-permute-start.12) | collective-permute-done | bytes 655392 | tf_op jit(solution)/shard_map/ppermute | solution.py:390
  93.5 2.0 collective-permute-start.9
  95.5 3.9 %collective-permute-start.1 = (f32[4,49,8,128]{3,2,1,0:T(8,128)}, f32[4,49,8,128]{3,2,1,0:T(8,128)}, u32[]{:S(2)}, u32[]{:S(2)}) collective-permute-start(f32[4,49,8,128]{3,2,1,0:T(8,128)} %get-tuple-element.40), channel_id=1, source_target_pairs={{0,8},{1,9},{2,10},{3,11},{4,12},{5,13},{6,14},{7,15},{8,0},{9,1},... | collective-permute-start | bytes 2408456 | tf_op jit(solution)/shard_map/ppermute | solution.py:397
  100.1 1.6 collective-permute-start.13
  101.7 11.1 %collective-permute-done.9.refs_5_ = f32[16,80,128]{2,1,0:T(8,128)S(1)} collective-permute-done((f32[16,80,128]{2,1,0:T(8,128)}, f32[16,80,128]{2,1,0:T(8,128)S(1)}, u32[]{:S(2)}, u32[]{:S(2)}) %collective-permute-start.9) | collective-permute-done | bytes 655392 | tf_op jit(solution)/shard_map/ppermute | solution.py:390
  112.8 3.2 %collective-permute-start.14 = (f32[4,64,8,128]{3,2,1,0:T(8,128)}, f32[4,64,8,128]{3,2,1,0:T(8,128)S(1)}, u32[]{:S(2)}, u32[]{:S(2)}) collective-permute-start(f32[4,64,8,128]{3,2,1,0:T(8,128)} %get-tuple-element.56), channel_id=1, source_target_pairs={{0,2},{1,3},{2,0},{3,1},{4,6},{5,7},{6,4},{7,5},{8,10},{9,11},{10,... | collective-permute-start | bytes 3145736 | tf_op jit(solution)/shard_map/ppermute | solution.py:397
  116.0 0.9 copy-done.6
  116.9 1.1 collective-permute-start.15
  118.7 5.9 %weigh.1 = f32[16,4,80,128]{3,2,1,0:T(8,128)} custom-call(f32[32]{0:T(128)} %reshape.10.refs_0_.refs_1_, f32[16,80,128]{2,1,0:T(8,128)} %get-tuple-element.46.refs_1_, f32[16,80,128]{2,1,0:T(8,128)} %copy-done.13, f32[16,80,128]{2,1,0:T(8,128)} %copy-done.14, f32[16,80,128]{2,1,0:T(8,128)} %copy-done.15, f32[16,80,128]{2,1,0:T(8,128)} %copy-done.16, ...), custom_call_target="tpu_custom_call" | custom-call | tf_op jit(solution)/shard_map/weigh/pallas_call | solution.py:192
  124.7 6.6 %all-to-all-start = ((f32[16,4,80,128]{3,2,1,0:T(8,128)}), f32[16,4,80,128]{3,2,1,0:T(8,128)}, u32[]{:S(2)}, u32[]{:S(2)}) async-start(f32[16,4,80,128]{3,2,1,0:T(8,128)} %weigh.1), calls=%async_computation | async-start | bytes 5242880 | tf_op jit(solution)/shard_map/all_to_all | solution.py:424
  131.3 5.4 %collective-permute-done.2.refs_3_.refs_4_ = f32[4,49,8,128]{3,2,1,0:T(8,128)} collective-permute-done((f32[4,49,8,128]{3,2,1,0:T(8,128)}, f32[4,49,8,128]{3,2,1,0:T(8,128)}, u32[]{:S(2)}, u32[]{:S(2)}) %collective-permute-start.2) | collective-permute-done | bytes 802848 | tf_op jit(solution)/shard_map/ppermute | solution.py:397
  136.6 2.8 turn.2
  139.4 1.6 collective-permute-start.3
  141.1 2.9 collective-permute-start.4
  144.0 1.3 collective-permute-start.5
  145.3 6.0 %collective-permute-done.14.refs_2_.refs_10_ = f32[4,64,8,128]{3,2,1,0:T(8,128)S(1)} collective-permute-done((f32[4,64,8,128]{3,2,1,0:T(8,128)}, f32[4,64,8,128]{3,2,1,0:T(8,128)S(1)}, u32[]{:S(2)}, u32[]{:S(2)}) %collective-permute-start.14) | collective-permute-done | bytes 1048608 | tf_op jit(solution)/shard_map/ppermute | solution.py:397
  151.4 12.1 %collective-permute-done.15.refs_3_.refs_11_ = f32[4,64,8,128]{3,2,1,0:T(8,128)S(1)} collective-permute-done((f32[4,64,8,128]{3,2,1,0:T(8,128)}, f32[4,64,8,128]{3,2,1,0:T(8,128)S(1)}, u32[]{:S(2)}, u32[]{:S(2)}) %collective-permute-start.15) | collective-permute-done | bytes 1048608 | tf_op jit(solution)/shard_map/ppermute | solution.py:397
  163.4 1.0 copy-done.5
  164.4 2.9 turn.3
  167.4 2.0 collective-permute-start.16
  169.3 3.6 %collective-permute-start.17 = (f32[4,64,8,128]{3,2,1,0:T(8,128)}, f32[4,64,8,128]{3,2,1,0:T(8,128)S(1)}, u32[]{:S(2)}, u32[]{:S(2)}) collective-permute-start(f32[4,64,8,128]{3,2,1,0:T(8,128)} %get-tuple-element.59), channel_id=1, source_target_pairs={{0,8},{1,9},{2,10},{3,11},{4,12},{5,13},{6,14},{7,15},{8,0},{9,1},... | collective-permute-start | bytes 3145736 | tf_op jit(solution)/shard_map/ppermute | solution.py:397
  172.9 25.0 %collective-permute-done.3.refs_5_ = f32[4,49,8,128]{3,2,1,0:T(8,128)} collective-permute-done((f32[4,49,8,128]{3,2,1,0:T(8,128)}, f32[4,49,8,128]{3,2,1,0:T(8,128)}, u32[]{:S(2)}, u32[]{:S(2)}) %collective-permute-start.3) | collective-permute-done | bytes 802848 | tf_op jit(solution)/shard_map/ppermute | solution.py:397
  197.9 3.1 %collective-permute-start.18 = (f32[4,64,8,128]{3,2,1,0:T(8,128)}, f32[4,64,8,128]{3,2,1,0:T(8,128)S(1)}, u32[]{:S(2)}, u32[]{:S(2)}) collective-permute-start(f32[4,64,8,128]{3,2,1,0:T(8,128)} %get-tuple-element.60), channel_id=1, source_target_pairs={{0,12},{1,13},{2,14},{3,15},{4,0},{5,1},{6,2},{7,3},{8,4},{9,5},{1... | collective-permute-start | bytes 3145736 | tf_op jit(solution)/shard_map/ppermute | solution.py:397
  203.8 0.7 slice.31
  204.5 14.6 %collective-permute-done.4.refs_6_ = f32[4,49,8,128]{3,2,1,0:T(8,128)} collective-permute-done((f32[4,49,8,128]{3,2,1,0:T(8,128)}, f32[4,49,8,128]{3,2,1,0:T(8,128)}, u32[]{:S(2)}, u32[]{:S(2)}) %collective-permute-start.4) | collective-permute-done | bytes 802848 | tf_op jit(solution)/shard_map/ppermute | solution.py:397
  219.1 0.7 slice.32
  219.8 8.3 %collective-permute-done.5.refs_7_ = f32[4,49,8,128]{3,2,1,0:T(8,128)} collective-permute-done((f32[4,49,8,128]{3,2,1,0:T(8,128)}, f32[4,49,8,128]{3,2,1,0:T(8,128)}, u32[]{:S(2)}, u32[]{:S(2)}) %collective-permute-start.5) | collective-permute-done | bytes 802848 | tf_op jit(solution)/shard_map/ppermute | solution.py:397
  228.1 0.7 slice.33
  229.5 0.9 copy-done.7
  231.0 10.4 %add_tile_first.1 = (f32[512,128]{1,0:T(8,128)}, f32[512,128]{1,0:T(8,128)}, f32[512,128]{1,0:T(8,128)}, f32[512,128]{1,0:T(8,128)}, f32[512,128]{1,0:T(8,128)},...) custom-call(s32[4096]{0:T(1024)} %bitcast.18, f32[4,49,8,128]{3,2,1,0:T(8,128)} %get-tuple-element.38.refs_0_.refs_1_, ...), custom_call_target="tpu_custom_call" | custom-call | tf_op jit(solution)/shard_map/add_tile_first/pallas_call | solution.py:262
  241.7 4.4 %collective-permute-start.22 = (f32[512,128]{1,0:T(8,128)}, f32[512,128]{1,0:T(8,128)S(1)}, u32[]{:S(2)}, u32[]{:S(2)}) collective-permute-start(f32[512,128]{1,0:T(8,128)} %get-tuple-element.65), channel_id=1, source_target_pairs={{0,64},{16,80},{32,96},{48,112},{64,0},{80,16},{96,32},{112,48},{1... | collective-permute-start | bytes 786440 | tf_op jit(solution)/shard_map/ppermute | solution.py:390
  246.0 1.8 collective-permute-start.24
  247.9 4.3 %collective-permute-done.20.refs_5_ = f32[512,128]{1,0:T(8,128)S(1)} collective-permute-done((f32[512,128]{1,0:T(8,128)}, f32[512,128]{1,0:T(8,128)S(1)}, u32[]{:S(2)}, u32[]{:S(2)}) %collective-permute-start.20) | collective-permute-done | bytes 262176 | tf_op jit(solution)/shard_map/ppermute | solution.py:390
  252.2 15.8 %collective-permute-done.21.refs_6_ = f32[512,128]{1,0:T(8,128)S(1)} collective-permute-done((f32[512,128]{1,0:T(8,128)}, f32[512,128]{1,0:T(8,128)S(1)}, u32[]{:S(2)}, u32[]{:S(2)}) %collective-permute-start.21) | collective-permute-done | bytes 262176 | tf_op jit(solution)/shard_map/ppermute | solution.py:390
  268.4 0.9 copy-done
  269.3 7.1 %finish.1 = f32[16,4,32,128]{3,2,1,0:T(8,128)S(1)} custom-call(s32[4096]{0:T(1024)S(1)} %bitcast.19, f32[32]{0:T(128)S(1)} %copy-done.2, f32[16,4,80,128]{3,2,1,0:T(8,128)} %all-to-all-done.refs_2_, f32[512,128]{1,0:T(8,128)S(1)} %copy-done, f32[512,128]{1,0:T(8,128)S(1)} %collective-permute-done.19.refs_4_, f32[512,128]{1,0:T(8,128)S(1)} %collective-permute-done.20.refs_5_, ...), custom_call_target="tpu_custom_call" | custom-call | tf_op jit(solution)/shard_map/finish/pallas_call | solution.py:336
  276.4 26.3 %all_to_all.10 = f32[16,4,32,128]{3,2,1,0:T(8,128)S(1)} all-to-all(f32[16,4,32,128]{3,2,1,0:T(8,128)S(1)} %finish.1), channel_id=1, replica_groups=mesh['tau'=8,'tile'=16] {'tile'}, dimensions={0} | all-to-all | bytes 2097152 | tf_op jit(solution)/shard_map/all_to_all | solution.py:433
  302.7 1.6 copy.7
  (65 shorter events, 7.7 us)
Async XLA Ops:
  26.5 39.4 %copy-start.18 = (f32[4,49,8,128]{3,2,1,0:T(8,128)S(1)}, f32[4,49,8,128]{3,2,1,0:T(8,128)}, u32[]{:S(2)}) copy-start(f32[4,49,8,128]{3,2,1,0:T(8,128)} %get-tuple-element.39) | copy-start | bytes 2408452
  26.6 91.5 %copy-start.17 = (f32[4,8]{1,0:T(4,128)S(1)}, f32[4,8]{1,0:T(4,128)}, u32[]{:S(2)}) copy-start(f32[4,8]{1,0:T(4,128)} %param.8) | copy-start | bytes 388
  46.3 18.7 %collective-permute-start.10 = (f32[16,80,128]{2,1,0:T(8,128)}, f32[16,80,128]{2,1,0:T(8,128)S(1)}, u32[]{:S(2)}, u32[]{:S(2)}) collective-permute-start(f32[16,80,128]{2,1,0:T(8,128)} %get-tuple-element.51), channel_id=1, source_target_pairs={{0,80},{16,64},{32,112},{48,96},{64,16},{80,0},{96,48},{112,32},{1... | collective-permute-start | bytes 1966088 | tf_op jit(solution)/shard_map/ppermute | solution.py:390
  49.0 30.5 %collective-permute-start.11 = (f32[16,80,128]{2,1,0:T(8,128)}, f32[16,80,128]{2,1,0:T(8,128)S(1)}, u32[]{:S(2)}, u32[]{:S(2)}) collective-permute-start(f32[16,80,128]{2,1,0:T(8,128)} %get-tuple-element.52), channel_id=1, source_target_pairs={{0,96},{16,112},{32,0},{48,16},{64,32},{80,48},{96,64},{112,80},{1... | collective-permute-start | bytes 1966088 | tf_op jit(solution)/shard_map/ppermute | solution.py:390
  50.1 43.3 %collective-permute-start.12 = (f32[16,80,128]{2,1,0:T(8,128)}, f32[16,80,128]{2,1,0:T(8,128)S(1)}, u32[]{:S(2)}, u32[]{:S(2)}) collective-permute-start(f32[16,80,128]{2,1,0:T(8,128)} %get-tuple-element.53), channel_id=1, source_target_pairs={{0,112},{16,96},{32,16},{48,0},{64,48},{80,32},{96,80},{112,64},{1... | collective-permute-start | bytes 1966088 | tf_op jit(solution)/shard_map/ppermute | solution.py:390
  50.4 45.1 %collective-permute-start.6 = (f32[16,80,128]{2,1,0:T(8,128)}, f32[16,80,128]{2,1,0:T(8,128)S(1)}, u32[]{:S(2)}, u32[]{:S(2)}) collective-permute-start(f32[16,80,128]{2,1,0:T(8,128)} %get-tuple-element.47), channel_id=1, source_target_pairs={{0,16},{16,0},{32,48},{48,32},{64,80},{80,64},{96,112},{112,96},{1... | collective-permute-start | bytes 1966088 | tf_op jit(solution)/shard_map/ppermute | solution.py:390
  50.5 48.8 %collective-permute-start.7 = (f32[16,80,128]{2,1,0:T(8,128)}, f32[16,80,128]{2,1,0:T(8,128)S(1)}, u32[]{:S(2)}, u32[]{:S(2)}) collective-permute-start(f32[16,80,128]{2,1,0:T(8,128)} %get-tuple-element.48), channel_id=1, source_target_pairs={{0,32},{16,48},{32,64},{48,80},{64,96},{80,112},{96,0},{112,16},{1... | collective-permute-start | bytes 1966088 | tf_op jit(solution)/shard_map/ppermute | solution.py:390
  65.1 0.8 copy-start.10
  65.9 50.1 %collective-permute-start = (f32[4,49,8,128]{3,2,1,0:T(8,128)S(1)}, f32[4,49,8,128]{3,2,1,0:T(8,128)S(1)}, u32[]{:S(2)}, u32[]{:S(2)}) collective-permute-start(f32[4,49,8,128]{3,2,1,0:T(8,128)S(1)} %copy-done.18), channel_id=1, source_target_pairs={{0,4},{1,5},{2,6},{3,7},{4,8},{5,9},{6,10},{7,11},{8,12},{9,13},{1... | collective-permute-start | bytes 2408456 | tf_op jit(solution)/shard_map/ppermute | solution.py:397
  79.5 37.5 %copy-start.11 = (f32[16,80,128]{2,1,0:T(8,128)}, f32[16,80,128]{2,1,0:T(8,128)S(1)}, u32[]{:S(2)}) copy-start(f32[16,80,128]{2,1,0:T(8,128)S(1)} %collective-permute-done.11.refs_7_) | copy-start | bytes 1966084
  79.5 20.6 %collective-permute-start.8 = (f32[16,80,128]{2,1,0:T(8,128)}, f32[16,80,128]{2,1,0:T(8,128)S(1)}, u32[]{:S(2)}, u32[]{:S(2)}) collective-permute-start(f32[16,80,128]{2,1,0:T(8,128)} %get-tuple-element.49), channel_id=1, source_target_pairs={{0,48},{16,32},{32,80},{48,64},{64,112},{80,96},{96,16},{112,0},{1... | collective-permute-start | bytes 1966088 | tf_op jit(solution)/shard_map/ppermute | solution.py:390
  93.5 23.4 %copy-start.12 = (f32[16,80,128]{2,1,0:T(8,128)}, f32[16,80,128]{2,1,0:T(8,128)S(1)}, u32[]{:S(2)}) copy-start(f32[16,80,128]{2,1,0:T(8,128)S(1)} %collective-permute-done.12.refs_8_) | copy-start | bytes 1966084
  93.5 19.3 %collective-permute-start.9 = (f32[16,80,128]{2,1,0:T(8,128)}, f32[16,80,128]{2,1,0:T(8,128)S(1)}, u32[]{:S(2)}, u32[]{:S(2)}) collective-permute-start(f32[16,80,128]{2,1,0:T(8,128)} %get-tuple-element.50), channel_id=1, source_target_pairs={{0,64},{16,80},{32,96},{48,112},{64,0},{80,16},{96,32},{112,48},{1... | collective-permute-start | bytes 1966088 | tf_op jit(solution)/shard_map/ppermute | solution.py:390
  95.5 21.4 %copy-start.13 = (f32[16,80,128]{2,1,0:T(8,128)}, f32[16,80,128]{2,1,0:T(8,128)S(1)}, u32[]{:S(2)}) copy-start(f32[16,80,128]{2,1,0:T(8,128)S(1)} %collective-permute-done.6.refs_2_) | copy-start | bytes 1966084
  95.5 35.8 %collective-permute-start.1 = (f32[4,49,8,128]{3,2,1,0:T(8,128)}, f32[4,49,8,128]{3,2,1,0:T(8,128)}, u32[]{:S(2)}, u32[]{:S(2)}) collective-permute-start(f32[4,49,8,128]{3,2,1,0:T(8,128)} %get-tuple-element.40), channel_id=1, source_target_pairs={{0,8},{1,9},{2,10},{3,11},{4,12},{5,13},{6,14},{7,15},{8,0},{9,1},... | collective-permute-start | bytes 2408456 | tf_op jit(solution)/shard_map/ppermute | solution.py:397
  99.4 17.5 %copy-start.14 = (f32[16,80,128]{2,1,0:T(8,128)}, f32[16,80,128]{2,1,0:T(8,128)S(1)}, u32[]{:S(2)}) copy-start(f32[16,80,128]{2,1,0:T(8,128)S(1)} %collective-permute-done.7.refs_3_) | copy-start | bytes 1966084
  99.4 37.3 %collective-permute-start.2 = (f32[4,49,8,128]{3,2,1,0:T(8,128)}, f32[4,49,8,128]{3,2,1,0:T(8,128)}, u32[]{:S(2)}, u32[]{:S(2)}) collective-permute-start(f32[4,49,8,128]{3,2,1,0:T(8,128)} %get-tuple-element.41), channel_id=1, source_target_pairs={{0,12},{1,13},{2,14},{3,15},{4,0},{5,1},{6,2},{7,3},{8,4},{9,5},{1... | collective-permute-start | bytes 2408456 | tf_op jit(solution)/shard_map/ppermute | solution.py:397
  100.1 16.8 %copy-start.15 = (f32[16,80,128]{2,1,0:T(8,128)}, f32[16,80,128]{2,1,0:T(8,128)S(1)}, u32[]{:S(2)}) copy-start(f32[16,80,128]{2,1,0:T(8,128)S(1)} %collective-permute-done.8.refs_4_) | copy-start | bytes 1966084
  100.1 43.9 %collective-permute-start.13 = (f32[4,64,8,128]{3,2,1,0:T(8,128)}, f32[4,64,8,128]{3,2,1,0:T(8,128)S(1)}, u32[]{:S(2)}, u32[]{:S(2)}) collective-permute-start(f32[4,64,8,128]{3,2,1,0:T(8,128)} %get-tuple-element.55), channel_id=1, source_target_pairs={{0,1},{1,2},{2,3},{3,0},{4,5},{5,6},{6,7},{7,4},{8,9},{9,10},{10,1... | collective-permute-start | bytes 3145736 | tf_op jit(solution)/shard_map/ppermute | solution.py:397
  112.8 4.1 %copy-start.16 = (f32[16,80,128]{2,1,0:T(8,128)}, f32[16,80,128]{2,1,0:T(8,128)S(1)}, u32[]{:S(2)}) copy-start(f32[16,80,128]{2,1,0:T(8,128)S(1)} %collective-permute-done.9.refs_5_) | copy-start | bytes 1966084
  112.8 38.5 %collective-permute-start.14 = (f32[4,64,8,128]{3,2,1,0:T(8,128)}, f32[4,64,8,128]{3,2,1,0:T(8,128)S(1)}, u32[]{:S(2)}, u32[]{:S(2)}) collective-permute-start(f32[4,64,8,128]{3,2,1,0:T(8,128)} %get-tuple-element.56), channel_id=1, source_target_pairs={{0,2},{1,3},{2,0},{3,1},{4,6},{5,7},{6,4},{7,5},{8,10},{9,11},{10,... | collective-permute-start | bytes 3145736 | tf_op jit(solution)/shard_map/ppermute | solution.py:397
  116.0 0.9 copy-start.6
  116.9 46.5 %collective-permute-start.15 = (f32[4,64,8,128]{3,2,1,0:T(8,128)}, f32[4,64,8,128]{3,2,1,0:T(8,128)S(1)}, u32[]{:S(2)}, u32[]{:S(2)}) collective-permute-start(f32[4,64,8,128]{3,2,1,0:T(8,128)} %get-tuple-element.57), channel_id=1, source_target_pairs={{0,3},{1,0},{2,1},{3,2},{4,7},{5,4},{6,5},{7,6},{8,11},{9,8},{10,9... | collective-permute-start | bytes 3145736 | tf_op jit(solution)/shard_map/ppermute | solution.py:397
  124.7 143.7 %all-to-all-start = ((f32[16,4,80,128]{3,2,1,0:T(8,128)}), f32[16,4,80,128]{3,2,1,0:T(8,128)}, u32[]{:S(2)}, u32[]{:S(2)}) async-start(f32[16,4,80,128]{3,2,1,0:T(8,128)} %weigh.1), calls=%async_computation | async-start | bytes 5242880 | tf_op jit(solution)/shard_map/all_to_all | solution.py:424
  139.4 58.5 %collective-permute-start.3 = (f32[4,49,8,128]{3,2,1,0:T(8,128)}, f32[4,49,8,128]{3,2,1,0:T(8,128)}, u32[]{:S(2)}, u32[]{:S(2)}) collective-permute-start(f32[4,49,8,128]{3,2,1,0:T(8,128)} %get-tuple-element.42), channel_id=1, source_target_pairs={{0,1},{1,2},{2,3},{3,0},{4,5},{5,6},{6,7},{7,4},{8,9},{9,10},{10,1... | collective-permute-start | bytes 2408456 | tf_op jit(solution)/shard_map/ppermute | solution.py:397
  141.1 78.1 %collective-permute-start.4 = (f32[4,49,8,128]{3,2,1,0:T(8,128)}, f32[4,49,8,128]{3,2,1,0:T(8,128)}, u32[]{:S(2)}, u32[]{:S(2)}) collective-permute-start(f32[4,49,8,128]{3,2,1,0:T(8,128)} %get-tuple-element.43), channel_id=1, source_target_pairs={{0,2},{1,3},{2,0},{3,1},{4,6},{5,7},{6,4},{7,5},{8,10},{9,11},{10,... | collective-permute-start | bytes 2408456 | tf_op jit(solution)/shard_map/ppermute | solution.py:397
  144.0 19.5 %copy-start.3 = (f32[4,64,8,128]{3,2,1,0:T(8,128)}, f32[4,64,8,128]{3,2,1,0:T(8,128)S(1)}, u32[]{:S(2)}) copy-start(f32[4,64,8,128]{3,2,1,0:T(8,128)S(1)} %collective-permute-done.13.refs_1_.refs_9_) | copy-start | bytes 3145732
  144.0 84.1 %collective-permute-start.5 = (f32[4,49,8,128]{3,2,1,0:T(8,128)}, f32[4,49,8,128]{3,2,1,0:T(8,128)}, u32[]{:S(2)}, u32[]{:S(2)}) collective-permute-start(f32[4,49,8,128]{3,2,1,0:T(8,128)} %get-tuple-element.44), channel_id=1, source_target_pairs={{0,3},{1,0},{2,1},{3,2},{4,7},{5,4},{6,5},{7,6},{8,11},{9,8},{10,9... | collective-permute-start | bytes 2408456 | tf_op jit(solution)/shard_map/ppermute | solution.py:397
  151.4 12.1 %copy-start.4 = (f32[4,64,8,128]{3,2,1,0:T(8,128)}, f32[4,64,8,128]{3,2,1,0:T(8,128)S(1)}, u32[]{:S(2)}) copy-start(f32[4,64,8,128]{3,2,1,0:T(8,128)S(1)} %collective-permute-done.14.refs_2_.refs_10_) | copy-start | bytes 3145732
  163.4 1.0 copy-start.5
  167.4 62.1 %collective-permute-start.16 = (f32[4,64,8,128]{3,2,1,0:T(8,128)}, f32[4,64,8,128]{3,2,1,0:T(8,128)S(1)}, u32[]{:S(2)}, u32[]{:S(2)}) collective-permute-start(f32[4,64,8,128]{3,2,1,0:T(8,128)} %get-tuple-element.58), channel_id=1, source_target_pairs={{0,4},{1,5},{2,6},{3,7},{4,8},{5,9},{6,10},{7,11},{8,12},{9,13},{1... | collective-permute-start | bytes 3145736 | tf_op jit(solution)/shard_map/ppermute | solution.py:397
  169.3 60.1 %collective-permute-start.17 = (f32[4,64,8,128]{3,2,1,0:T(8,128)}, f32[4,64,8,128]{3,2,1,0:T(8,128)S(1)}, u32[]{:S(2)}, u32[]{:S(2)}) collective-permute-start(f32[4,64,8,128]{3,2,1,0:T(8,128)} %get-tuple-element.59), channel_id=1, source_target_pairs={{0,8},{1,9},{2,10},{3,11},{4,12},{5,13},{6,14},{7,15},{8,0},{9,1},... | collective-permute-start | bytes 3145736 | tf_op jit(solution)/shard_map/ppermute | solution.py:397
  197.9 31.5 %collective-permute-start.18 = (f32[4,64,8,128]{3,2,1,0:T(8,128)}, f32[4,64,8,128]{3,2,1,0:T(8,128)S(1)}, u32[]{:S(2)}, u32[]{:S(2)}) collective-permute-start(f32[4,64,8,128]{3,2,1,0:T(8,128)} %get-tuple-element.60), channel_id=1, source_target_pairs={{0,12},{1,13},{2,14},{3,15},{4,0},{5,1},{6,2},{7,3},{8,4},{9,5},{1... | collective-permute-start | bytes 3145736 | tf_op jit(solution)/shard_map/ppermute | solution.py:397
  229.4 1.0 copy-start.7
  229.4 1.3 copy-start.8
  229.4 1.6 copy-start.9
  231.0 37.3 %copy-start.1 = (s32[4,4,2,128]{3,2,1,0:T(2,128)S(1)}, s32[4,4,2,128]{3,2,1,0:T(2,128)}, u32[]{:S(2)}) copy-start(s32[4,4,2,128]{3,2,1,0:T(2,128)} %maximum_convert_fusion) | copy-start | bytes 49156
  231.0 37.3 %copy-start.2 = (f32[32]{0:T(128)S(1)}, f32[32]{0:T(128)}, u32[]{:S(2)}) copy-start(f32[32]{0:T(128)} %reshape.10.refs_0_.refs_1_) | copy-start | bytes 388
  241.5 4.6 %collective-permute-start.19 = (f32[512,128]{1,0:T(8,128)}, f32[512,128]{1,0:T(8,128)S(1)}, u32[]{:S(2)}, u32[]{:S(2)}) collective-permute-start(f32[512,128]{1,0:T(8,128)} %get-tuple-element.62), channel_id=1, source_target_pairs={{0,16},{16,0},{32,48},{48,32},{64,80},{80,64},{96,112},{112,96},{1... | collective-permute-start | bytes 786440 | tf_op jit(solution)/shard_map/ppermute | solution.py:390
  241.5 10.7 %collective-permute-start.20 = (f32[512,128]{1,0:T(8,128)}, f32[512,128]{1,0:T(8,128)S(1)}, u32[]{:S(2)}, u32[]{:S(2)}) collective-permute-start(f32[512,128]{1,0:T(8,128)} %get-tuple-element.63), channel_id=1, source_target_pairs={{0,32},{16,48},{32,64},{48,80},{64,96},{80,112},{96,0},{112,16},{1... | collective-permute-start | bytes 786440 | tf_op jit(solution)/shard_map/ppermute | solution.py:390
  241.6 26.4 %collective-permute-start.21 = (f32[512,128]{1,0:T(8,128)}, f32[512,128]{1,0:T(8,128)S(1)}, u32[]{:S(2)}, u32[]{:S(2)}) collective-permute-start(f32[512,128]{1,0:T(8,128)} %get-tuple-element.64), channel_id=1, source_target_pairs={{0,48},{16,32},{32,80},{48,64},{64,112},{80,96},{96,16},{112,0},{1... | collective-permute-start | bytes 786440 | tf_op jit(solution)/shard_map/ppermute | solution.py:390
  241.7 26.3 %collective-permute-start.22 = (f32[512,128]{1,0:T(8,128)}, f32[512,128]{1,0:T(8,128)S(1)}, u32[]{:S(2)}, u32[]{:S(2)}) collective-permute-start(f32[512,128]{1,0:T(8,128)} %get-tuple-element.65), channel_id=1, source_target_pairs={{0,64},{16,80},{32,96},{48,112},{64,0},{80,16},{96,32},{112,48},{1... | collective-permute-start | bytes 786440 | tf_op jit(solution)/shard_map/ppermute | solution.py:390
  246.0 21.9 %collective-permute-start.23 = (f32[512,128]{1,0:T(8,128)}, f32[512,128]{1,0:T(8,128)S(1)}, u32[]{:S(2)}, u32[]{:S(2)}) collective-permute-start(f32[512,128]{1,0:T(8,128)} %get-tuple-element.66), channel_id=1, source_target_pairs={{0,80},{16,64},{32,112},{48,96},{64,16},{80,0},{96,48},{112,32},{1... | collective-permute-start | bytes 786440 | tf_op jit(solution)/shard_map/ppermute | solution.py:390
  246.0 21.9 %collective-permute-start.24 = (f32[512,128]{1,0:T(8,128)}, f32[512,128]{1,0:T(8,128)S(1)}, u32[]{:S(2)}, u32[]{:S(2)}) collective-permute-start(f32[512,128]{1,0:T(8,128)} %get-tuple-element.67), channel_id=1, source_target_pairs={{0,96},{16,112},{32,0},{48,16},{64,32},{80,48},{96,64},{112,80},{1... | collective-permute-start | bytes 786440 | tf_op jit(solution)/shard_map/ppermute | solution.py:390
  252.2 16.2 %collective-permute-start.25 = (f32[512,128]{1,0:T(8,128)}, f32[512,128]{1,0:T(8,128)S(1)}, u32[]{:S(2)}, u32[]{:S(2)}) collective-permute-start(f32[512,128]{1,0:T(8,128)} %get-tuple-element.68), channel_id=1, source_target_pairs={{0,112},{16,96},{32,16},{48,0},{64,48},{80,32},{96,80},{112,64},{1... | collective-permute-start | bytes 786440 | tf_op jit(solution)/shard_map/ppermute | solution.py:390
  268.3 1.0 copy-start
where the time goes:
time: 306 us; the launch traced here: 304 us
  waiting for transfers between devices  140 us (46%)
  Pallas kernels  74.2 us (24%)
  starting transfers between devices  49.2 us (16%)
  blocking collectives  26.3 us (9%)
  local copies, waits for them, and re-layouts  13 us (4%)
    ppermute x12, waiting for transfers between devices, over_tile(): lax.ppermute(rows, 'tile', [(i, around(i, s, u, z_first)) for i in range(...  71.4 us
    ppermute x14, waiting for transfers between devices, over_tau(): lax.ppermute(strip, 'tau', [(i, partner(i, shift, ntau)) for i in range(n...  68.8 us
    ppermute x12, starting transfers between devices, over_tile(): lax.ppermute(rows, 'tile', [(i, around(i, s, u, z_first)) for i in range(...  27.2 us
    all_to_all x1, blocking collectives, body(): owned = lax.all_to_all(spectrum, 'tile', 0, 0, tiled=True)  26.3 us
    pallas_call x1, Pallas kernels, tile_first_products(): pl.pallas_call(kernel, out_shape=[jax.ShapeDtypeStruct((SIDE, n, SUB, TIL...  25.3 us
    pallas_call x1, Pallas kernels, tau_first_products(): pl.pallas_call(kernel, out_shape=[jax.ShapeDtypeStruct((STRIP, count, TIL...  19.8 us
    ppermute x14, starting transfers between devices, over_tau(): lax.ppermute(strip, 'tau', [(i, partner(i, shift, ntau)) for i in range(n...  15.4 us
    pallas_call x1, Pallas kernels, add_tile_first(): pl.pallas_call(kernel, out_shape=[jax.ShapeDtypeStruct((tiles, TILE), jnp...  10.4 us
  transfers between devices with their start and end apart: 27, of which 13 were waited for; matrix products, arithmetic and copies ran while one was open for 2% of the time, Pallas kernels for 7%

commit v1 on v0

--- a/solution.py
+++ b/solution.py
@@ -10,13 +10,15 @@
 SUB = 8
 CHI_DEV = 32
 STRIP = 16
-TILE_FIRST = (48, 64)
+TILE_FIRST = (56, 56)
 TAU_FIRST = 80
 SIDE = 4
 
 
 def shifts(ntau):
-    return [(s, h) for s in range(ntau // 2) for h in range(2)]
+    chips = ntau // 2
+    far_first = sorted(range(chips), key=lambda s: (s > 0, -min(s, chips - s)))
+    return [(s, h) for s in far_first for h in range(2)]
 
 
 def partner(me, shift, ntau, back=False):
@@ -221,21 +223,16 @@
 
             work.append((rows, bases, count))
     for u in range(SIDE):
-        first, second = work[u], work[u + SIDE]
-        both = (first[0] + second[0], first[1] + second[1])
-        middle, end = sorted((first[2] // SUB, second[2] // SUB))
-        longer = max(first, second, key=lambda item: item[2])
-        for (rows, bases), low, high in ((both, 0, middle), (longer[:2], middle, end)):
-
-            def add(g, carry, rows=rows, bases=bases):
-                for q in range(SUB):
-                    p = g * SUB + q
-                    for ref, base, acc in zip(rows, bases, sums):
-                        acc[target[base + p]] += ref[p]
-                return carry
-
-            if low < high:
-                lax.fori_loop(low, high, add, 0)
+        rows, bases = work[u][0] + work[u + SIDE][0], work[u][1] + work[u + SIDE][1]
+
+        def add(g, carry, rows=rows, bases=bases):
+            for q in range(SUB):
+                p = g * SUB + q
+                for ref, base, acc in zip(rows, bases, sums):
+                    acc[target[base + p]] += ref[p]
+            return carry
+
+        lax.fori_loop(0, work[u][2] // SUB, add, 0)
 
     def turn(g, carry):
         at = pl.multiple_of(g * SUB, SUB)

time: 306 us -> 288 us (0.941)
  waiting for transfers between devices: 140 us -> 124 us
  starting transfers between devices: 49.2 us -> 53.9 us
  blocking collectives: 26.3 us -> 22.5 us
    ppermute x14, starting transfers between devices: 15.4 us -> 26.7 us  [over_tau(): lax.ppermute(strip, 'tau', [(i, partner(i, shift, ntau)) for i in range(n...]
    ppermute x14, waiting for transfers between devices: 68.8 us -> 59.5 us  [over_tau(): lax.ppermute(strip, 'tau', [(i, partner(i, shift, ntau)) for i in range(n...]
    ppermute x12, waiting for transfers between devices: 71.4 us -> 64.9 us  [over_tile(): lax.ppermute(rows, 'tile', [(i, around(i, s, u, z_first)) for i in range(...]
    ppermute x12, starting transfers between devices: 27.2 us -> 22.2 us  [over_tile(): lax.ppermute(rows, 'tile', [(i, around(i, s, u, z_first)) for i in range(...]
    all_to_all x1, blocking collectives: 26.3 us -> 22.5 us  [body(): owned = lax.all_to_all(spectrum, 'tile', 0, 0, tiled=True)]
  transfers between devices with their start and end apart: 27 -> 27, of which waited for: 13 -> 14; matrix products, arithmetic and copies ran while one was open for 2% -> 2% of each run, Pallas kernels for 7% -> 15%
where the time goes in v1:
time: 288 us; the launch traced here: 287 us
  waiting for transfers between devices  124 us (43%)
  Pallas kernels  74.4 us (26%)
  starting transfers between devices  53.9 us (19%)
  blocking collectives  22.5 us (8%)
  local copies, waits for them, and re-layouts  10.1 us (4%)
    ppermute x12, waiting for transfers between devices, over_tile(): lax.ppermute(rows, 'tile', [(i, around(i, s, u, z_first)) for i in range(...  64.9 us
    ppermute x14, waiting for transfers between devices, over_tau(): lax.ppermute(strip, 'tau', [(i, partner(i, shift, ntau)) for i in range(n...  59.5 us
    ppermute x14, starting transfers between devices, over_tau(): lax.ppermute(strip, 'tau', [(i, partner(i, shift, ntau)) for i in range(n...  26.7 us
    pallas_call x1, Pallas kernels, tile_first_products(): pl.pallas_call(kernel, out_shape=[jax.ShapeDtypeStruct((SIDE, n, SUB, TIL...  25.2 us
    all_to_all x1, blocking collectives, body(): owned = lax.all_to_all(spectrum, 'tile', 0, 0, tiled=True)  22.5 us
    ppermute x12, starting transfers between devices, over_tile(): lax.ppermute(rows, 'tile', [(i, around(i, s, u, z_first)) for i in range(...  22.2 us
    pallas_call x1, Pallas kernels, tau_first_products(): pl.pallas_call(kernel, out_shape=[jax.ShapeDtypeStruct((STRIP, count, TIL...  19.8 us
    pallas_call x1, Pallas kernels, add_tile_first(): pl.pallas_call(kernel, out_shape=[jax.ShapeDtypeStruct((tiles, TILE), jnp...  10.3 us
  transfers between devices with their start and end apart: 27, of which 14 were waited for; matrix products, arithmetic and copies ran while one was open for 2% of the time, Pallas kernels for 15%

profile of v1, /device:TPU:0, one launch (start us, length us, event | category | flops | bytes accessed | tf_op | source)
XLA Modules:
  0.0 286.8 jit_solution(7501031618508191554)
XLA Ops:
  0.0 0.7 convert_element_type.12
  1.3 25.2 %tile_first_products.1 = (f32[4,57,8,128]{3,2,1,0:T(8,128)}, f32[4,57,8,128]{3,2,1,0:T(8,128)}, f32[4,57,8,128]{3,2,1,0:T(8,128)}, f32[4,57,8,128]{3,2,1,0:T(8,1...) custom-call(s32[16,192]{1,0:T(8,128)} %bitcast.25, ...), custom_call_target="tpu_custom_call" | custom-call | tf_op jit(solution)/shard_map/tile_first_products/pallas_call | solution.py:96
  26.5 2.1 collective-permute-start
  28.6 3.6 %collective-permute-start.1 = (f32[4,57,8,128]{3,2,1,0:T(8,128)}, f32[4,57,8,128]{3,2,1,0:T(8,128)S(1)}, u32[]{:S(2)}, u32[]{:S(2)}) collective-permute-start(f32[4,57,8,128]{3,2,1,0:T(8,128)} %get-tuple-element.40), channel_id=1, source_target_pairs={{0,8},{1,9},{2,10},{3,11},{4,12},{5,13},{6,14},{7,15},{8,0},{9,1},... | collective-permute-start | bytes 2801672 | tf_op jit(solution)/shard_map/ppermute | solution.py:394
  32.2 1.0 collective-permute-start.2
  33.2 19.8 %tau_first_products.1 = (f32[16,80,128]{2,1,0:T(8,128)}, f32[16,80,128]{2,1,0:T(8,128)}, f32[16,80,128]{2,1,0:T(8,128)}, f32[16,80,128]{2,1,0:T(8,128)}, f32[16,...) custom-call(s32[16,192]{1,0:T(8,128)} %bitcast.26, ...), custom_call_target="tpu_custom_call" | custom-call | tf_op jit(solution)/shard_map/tau_first_products/pallas_call | solution.py:146
  53.2 2.8 collective-permute-start.11
  55.9 15.5 %collective-permute-done.10.refs_6_ = f32[16,80,128]{2,1,0:T(8,128)S(1)} collective-permute-done((f32[16,80,128]{2,1,0:T(8,128)}, f32[16,80,128]{2,1,0:T(8,128)S(1)}, u32[]{:S(2)}, u32[]{:S(2)}) %collective-permute-start.10) | collective-permute-done | bytes 655392 | tf_op jit(solution)/shard_map/ppermute | solution.py:387
  71.6 1.0 collective-permute-start.6
  72.6 1.5 collective-permute-start.7
  74.1 1.4 collective-permute-start.8
  75.6 1.2 collective-permute-start.9
  76.7 3.0 %turn.2 = (f32[4,57,8,128]{3,2,1,0:T(8,128)}, f32[4,57,8,128]{3,2,1,0:T(8,128)}, f32[4,57,8,128]{3,2,1,0:T(8,128)}) custom-call(f32[4,57,8,128]{3,2,1,0:T(8,128)} %get-tuple-element.38.refs_0_.refs_1_, f32[4,57,8,128]{3,2,1,0:T(8,128)} %copy-done.3, f32[4,57,8,128]{3,2,1,0:T(8,128)} %copy-done.4, f32[4,57,8,128]{3,2,1,0:T(8,128)} %copy-done.5), custom_call_target="tpu_custom_call" | custom-call | tf_op jit(solution)/shard_map/turn/pallas_call | solution.py:369
  79.7 8.6 %collective-permute-done.12.refs_8_ = f32[16,80,128]{2,1,0:T(8,128)} collective-permute-done((f32[16,80,128]{2,1,0:T(8,128)}, f32[16,80,128]{2,1,0:T(8,128)}, u32[]{:S(2)}, u32[]{:S(2)}) %collective-permute-start.12) | collective-permute-done | bytes 655392 | tf_op jit(solution)/shard_map/ppermute | solution.py:387
  88.4 1.6 collective-permute-start.3
  90.0 1.6 collective-permute-start.13
  92.1 3.2 %collective-permute-start.14 = (f32[4,56,8,128]{3,2,1,0:T(8,128)}, f32[4,56,8,128]{3,2,1,0:T(8,128)S(1)}, u32[]{:S(2)}, u32[]{:S(2)}) collective-permute-start(f32[4,56,8,128]{3,2,1,0:T(8,128)} %get-tuple-element.56), channel_id=1, source_target_pairs={{0,2},{1,3},{2,0},{3,1},{4,6},{5,7},{6,4},{7,5},{8,10},{9,11},{10,... | collective-permute-start | bytes 2752520 | tf_op jit(solution)/shard_map/ppermute | solution.py:394
  95.3 9.1 %collective-permute-done.8.refs_4_ = f32[16,80,128]{2,1,0:T(8,128)} collective-permute-done((f32[16,80,128]{2,1,0:T(8,128)}, f32[16,80,128]{2,1,0:T(8,128)}, u32[]{:S(2)}, u32[]{:S(2)}) %collective-permute-start.8) | collective-permute-done | bytes 655392 | tf_op jit(solution)/shard_map/ppermute | solution.py:387
  104.4 3.0 %collective-permute-start.15 = (f32[4,56,8,128]{3,2,1,0:T(8,128)}, f32[4,56,8,128]{3,2,1,0:T(8,128)S(1)}, u32[]{:S(2)}, u32[]{:S(2)}) collective-permute-start(f32[4,56,8,128]{3,2,1,0:T(8,128)} %get-tuple-element.57), channel_id=1, source_target_pairs={{0,3},{1,0},{2,1},{3,2},{4,7},{5,4},{6,5},{7,6},{8,11},{9,8},{10,9... | collective-permute-start | bytes 2752520 | tf_op jit(solution)/shard_map/ppermute | solution.py:394
  108.1 11.1 %collective-permute-done.9.refs_5_ = f32[16,80,128]{2,1,0:T(8,128)} collective-permute-done((f32[16,80,128]{2,1,0:T(8,128)}, f32[16,80,128]{2,1,0:T(8,128)}, u32[]{:S(2)}, u32[]{:S(2)}) %collective-permute-start.9) | collective-permute-done | bytes 655392 | tf_op jit(solution)/shard_map/ppermute | solution.py:387
  119.2 5.9 %weigh.1 = f32[16,4,80,128]{3,2,1,0:T(8,128)} custom-call(f32[32]{0:T(128)} %reshape.10.refs_0_.refs_1_, f32[16,80,128]{2,1,0:T(8,128)} %get-tuple-element.46.refs_1_, f32[16,80,128]{2,1,0:T(8,128)} %collective-permute-done.6.refs_2_, f32[16,80,128]{2,1,0:T(8,128)} %collective-permute-done.7.refs_3_, f32[16,80,128]{2,1,0:T(8,128)} %collective-permute-done.8.refs_4_, ...), custom_call_target="tpu_custom_call" | custom-call | tf_op jit(solution)/shard_map/weigh/pallas_call | solution.py:194
  125.2 5.1 %all-to-all-start = ((f32[16,4,80,128]{3,2,1,0:T(8,128)}), f32[16,4,80,128]{3,2,1,0:T(8,128)}, u32[]{:S(2)}, u32[]{:S(2)}) async-start(f32[16,4,80,128]{3,2,1,0:T(8,128)} %weigh.1), calls=%async_computation | async-start | bytes 5242880 | tf_op jit(solution)/shard_map/all_to_all | solution.py:421
  130.3 2.8 collective-permute-done.13.refs_1_.refs_9_
  133.0 21.0 %collective-permute-done.14.refs_2_.refs_10_ = f32[4,56,8,128]{3,2,1,0:T(8,128)S(1)} collective-permute-done((f32[4,56,8,128]{3,2,1,0:T(8,128)}, f32[4,56,8,128]{3,2,1,0:T(8,128)S(1)}, u32[]{:S(2)}, u32[]{:S(2)}) %collective-permute-start.14) | collective-permute-done | bytes 917536 | tf_op jit(solution)/shard_map/ppermute | solution.py:394
  154.1 0.9 copy-done.7
  155.3 3.0 %turn.3 = (f32[4,56,8,128]{3,2,1,0:T(8,128)}, f32[4,56,8,128]{3,2,1,0:T(8,128)}, f32[4,56,8,128]{3,2,1,0:T(8,128)}) custom-call(f32[4,56,8,128]{3,2,1,0:T(8,128)} %get-tuple-element.54.refs_0_.refs_8_, f32[4,56,8,128]{3,2,1,0:T(8,128)} %copy-done.6, f32[4,56,8,128]{3,2,1,0:T(8,128)} %copy-done.7, f32[4,56,8,128]{3,2,1,0:T(8,128)} %copy-done.8), custom_call_target="tpu_custom_call" | custom-call | tf_op jit(solution)/shard_map/turn/pallas_call | solution.py:369
  158.2 1.2 collective-permute-start.16
  159.8 2.4 collective-permute-start.18
  162.2 2.2 collective-permute-start.4
  164.4 0.7 slice_bitcast_fusion.3
  167.1 0.7 slice.31
  167.8 36.4 %collective-permute-done.4.refs_6_ = f32[4,57,8,128]{3,2,1,0:T(8,128)S(1)} collective-permute-done((f32[4,57,8,128]{3,2,1,0:T(8,128)}, f32[4,57,8,128]{3,2,1,0:T(8,128)S(1)}, u32[]{:S(2)}, u32[]{:S(2)}) %collective-permute-start.4) | collective-permute-done | bytes 933920 | tf_op jit(solution)/shard_map/ppermute | solution.py:394
  205.0 4.3 %collective-permute-done.17.refs_13_ = f32[4,56,8,128]{3,2,1,0:T(8,128)S(1)} collective-permute-done((f32[4,56,8,128]{3,2,1,0:T(8,128)}, f32[4,56,8,128]{3,2,1,0:T(8,128)S(1)}, u32[]{:S(2)}, u32[]{:S(2)}) %collective-permute-start.17) | collective-permute-done | bytes 917536 | tf_op jit(solution)/shard_map/ppermute | solution.py:394
  210.3 1.0 copy-done.13
  211.2 10.3 %add_tile_first.1 = (f32[512,128]{1,0:T(8,128)}, f32[512,128]{1,0:T(8,128)}, f32[512,128]{1,0:T(8,128)}, f32[512,128]{1,0:T(8,128)}, f32[512,128]{1,0:T(8,128)},...) custom-call(s32[4096]{0:T(1024)} %bitcast.18, f32[4,57,8,128]{3,2,1,0:T(8,128)} %get-tuple-element.38.refs_0_.refs_1_, ...), custom_call_target="tpu_custom_call" | custom-call | tf_op jit(solution)/shard_map/add_tile_first/pallas_call | solution.py:259
  221.6 0.9 collective-permute-start.20
  222.5 2.4 collective-permute-start.21
  224.9 7.4 %collective-permute-start.22 = (f32[512,128]{1,0:T(8,128)}, f32[512,128]{1,0:T(8,128)S(1)}, u32[]{:S(2)}, u32[]{:S(2)}) collective-permute-start(f32[512,128]{1,0:T(8,128)} %get-tuple-element.65), channel_id=1, source_target_pairs={{0,32},{16,48},{32,64},{48,80},{64,96},{80,112},{96,0},{112,16},{1... | collective-permute-start | bytes 786440 | tf_op jit(solution)/shard_map/ppermute | solution.py:387
  232.3 2.9 %collective-permute-start.24 = (f32[512,128]{1,0:T(8,128)}, f32[512,128]{1,0:T(8,128)S(1)}, u32[]{:S(2)}, u32[]{:S(2)}) collective-permute-start(f32[512,128]{1,0:T(8,128)} %get-tuple-element.67), channel_id=1, source_target_pairs={{0,96},{16,112},{32,0},{48,16},{64,32},{80,48},{96,64},{112,80},{1... | collective-permute-start | bytes 786440 | tf_op jit(solution)/shard_map/ppermute | solution.py:387
  235.3 4.9 %collective-permute-start.25 = (f32[512,128]{1,0:T(8,128)}, f32[512,128]{1,0:T(8,128)S(1)}, u32[]{:S(2)}, u32[]{:S(2)}) collective-permute-start(f32[512,128]{1,0:T(8,128)} %get-tuple-element.68), channel_id=1, source_target_pairs={{0,112},{16,96},{32,16},{48,0},{64,48},{80,32},{96,80},{112,64},{1... | collective-permute-start | bytes 786440 | tf_op jit(solution)/shard_map/ppermute | solution.py:387
  240.1 3.1 %collective-permute-done.22.refs_7_ = f32[512,128]{1,0:T(8,128)S(1)} collective-permute-done((f32[512,128]{1,0:T(8,128)}, f32[512,128]{1,0:T(8,128)S(1)}, u32[]{:S(2)}, u32[]{:S(2)}) %collective-permute-start.22) | collective-permute-done | bytes 262176 | tf_op jit(solution)/shard_map/ppermute | solution.py:387
  243.3 5.6 %collective-permute-done.23.refs_8_ = f32[512,128]{1,0:T(8,128)S(1)} collective-permute-done((f32[512,128]{1,0:T(8,128)}, f32[512,128]{1,0:T(8,128)S(1)}, u32[]{:S(2)}, u32[]{:S(2)}) %collective-permute-start.23) | collective-permute-done | bytes 262176 | tf_op jit(solution)/shard_map/ppermute | solution.py:387
  248.8 1.3 collective-permute-done.24.refs_9_
  250.1 4.5 %collective-permute-done.25.refs_10_ = f32[512,128]{1,0:T(8,128)S(1)} collective-permute-done((f32[512,128]{1,0:T(8,128)}, f32[512,128]{1,0:T(8,128)S(1)}, u32[]{:S(2)}, u32[]{:S(2)}) %collective-permute-start.25) | collective-permute-done | bytes 262176 | tf_op jit(solution)/shard_map/ppermute | solution.py:387
  254.6 0.9 copy-done
  255.6 7.1 %finish.1 = f32[16,4,32,128]{3,2,1,0:T(8,128)S(1)} custom-call(s32[4096]{0:T(1024)S(1)} %bitcast.19, f32[32]{0:T(128)S(1)} %copy-done.2, f32[16,4,80,128]{3,2,1,0:T(8,128)} %all-to-all-done.refs_2_, f32[512,128]{1,0:T(8,128)S(1)} %copy-done, f32[512,128]{1,0:T(8,128)S(1)} %collective-permute-done.19.refs_4_, f32[512,128]{1,0:T(8,128)S(1)} %collective-permute-done.20.refs_5_, ...), custom_call_target="tpu_custom_call" | custom-call | tf_op jit(solution)/shard_map/finish/pallas_call | solution.py:333
  262.7 22.5 %all_to_all.10 = f32[16,4,32,128]{3,2,1,0:T(8,128)S(1)} all-to-all(f32[16,4,32,128]{3,2,1,0:T(8,128)S(1)} %finish.1), channel_id=1, replica_groups=mesh['tau'=8,'tile'=16] {'tile'}, dimensions={0} | all-to-all | bytes 2097152 | tf_op jit(solution)/shard_map/all_to_all | solution.py:430
  285.2 1.6 copy.7
  (61 shorter events, 6.5 us)
Async XLA Ops:
  26.5 46.1 %collective-permute-start = (f32[4,57,8,128]{3,2,1,0:T(8,128)}, f32[4,57,8,128]{3,2,1,0:T(8,128)S(1)}, u32[]{:S(2)}, u32[]{:S(2)}) collective-permute-start(f32[4,57,8,128]{3,2,1,0:T(8,128)} %get-tuple-element.39), channel_id=1, source_target_pairs={{0,4},{1,5},{2,6},{3,7},{4,8},{5,9},{6,10},{7,11},{8,12},{9,13},{1... | collective-permute-start | bytes 2801672 | tf_op jit(solution)/shard_map/ppermute | solution.py:394
  28.6 45.5 %collective-permute-start.1 = (f32[4,57,8,128]{3,2,1,0:T(8,128)}, f32[4,57,8,128]{3,2,1,0:T(8,128)S(1)}, u32[]{:S(2)}, u32[]{:S(2)}) collective-permute-start(f32[4,57,8,128]{3,2,1,0:T(8,128)} %get-tuple-element.40), channel_id=1, source_target_pairs={{0,8},{1,9},{2,10},{3,11},{4,12},{5,13},{6,14},{7,15},{8,0},{9,1},... | collective-permute-start | bytes 2801672 | tf_op jit(solution)/shard_map/ppermute | solution.py:394
  32.2 43.4 %collective-permute-start.2 = (f32[4,57,8,128]{3,2,1,0:T(8,128)}, f32[4,57,8,128]{3,2,1,0:T(8,128)S(1)}, u32[]{:S(2)}, u32[]{:S(2)}) collective-permute-start(f32[4,57,8,128]{3,2,1,0:T(8,128)} %get-tuple-element.41), channel_id=1, source_target_pairs={{0,12},{1,13},{2,14},{3,15},{4,0},{5,1},{6,2},{7,3},{8,4},{9,5},{1... | collective-permute-start | bytes 2801672 | tf_op jit(solution)/shard_map/ppermute | solution.py:394
  33.2 74.3 %copy-start.16 = (f32[4,8]{1,0:T(4,128)S(1)}, f32[4,8]{1,0:T(4,128)}, u32[]{:S(2)}) copy-start(f32[4,8]{1,0:T(4,128)} %param.8) | copy-start | bytes 388
  53.0 18.4 %collective-permute-start.10 = (f32[16,80,128]{2,1,0:T(8,128)}, f32[16,80,128]{2,1,0:T(8,128)S(1)}, u32[]{:S(2)}, u32[]{:S(2)}) collective-permute-start(f32[16,80,128]{2,1,0:T(8,128)} %get-tuple-element.51), channel_id=1, source_target_pairs={{0,48},{16,32},{32,80},{48,64},{64,112},{80,96},{96,16},{112,0},{1... | collective-permute-start | bytes 1966088 | tf_op jit(solution)/shard_map/ppermute | solution.py:387
  53.2 18.4 %collective-permute-start.11 = (f32[16,80,128]{2,1,0:T(8,128)}, f32[16,80,128]{2,1,0:T(8,128)S(1)}, u32[]{:S(2)}, u32[]{:S(2)}) collective-permute-start(f32[16,80,128]{2,1,0:T(8,128)} %get-tuple-element.52), channel_id=1, source_target_pairs={{0,96},{16,112},{32,0},{48,16},{64,32},{80,48},{96,64},{112,80},{1... | collective-permute-start | bytes 1966088 | tf_op jit(solution)/shard_map/ppermute | solution.py:387
  71.4 47.8 %copy-start.14 = (f32[16,80,128]{2,1,0:T(8,128)}, f32[16,80,128]{2,1,0:T(8,128)S(1)}, u32[]{:S(2)}) copy-start(f32[16,80,128]{2,1,0:T(8,128)S(1)} %collective-permute-done.10.refs_6_) | copy-start | bytes 1966084
  71.4 16.9 %collective-permute-start.12 = (f32[16,80,128]{2,1,0:T(8,128)}, f32[16,80,128]{2,1,0:T(8,128)}, u32[]{:S(2)}, u32[]{:S(2)}) collective-permute-start(f32[16,80,128]{2,1,0:T(8,128)} %get-tuple-element.53), channel_id=1, source_target_pairs={{0,112},{16,96},{32,16},{48,0},{64,48},{80,32},{96,80},{112,64},{1... | collective-permute-start | bytes 1966088 | tf_op jit(solution)/shard_map/ppermute | solution.py:387
  71.6 4.0 %copy-start.15 = (f32[16,80,128]{2,1,0:T(8,128)}, f32[16,80,128]{2,1,0:T(8,128)S(1)}, u32[]{:S(2)}) copy-start(f32[16,80,128]{2,1,0:T(8,128)S(1)} %collective-permute-done.11.refs_7_) | copy-start | bytes 1966084
  71.6 18.4 %collective-permute-start.6 = (f32[16,80,128]{2,1,0:T(8,128)}, f32[16,80,128]{2,1,0:T(8,128)}, u32[]{:S(2)}, u32[]{:S(2)}) collective-permute-start(f32[16,80,128]{2,1,0:T(8,128)} %get-tuple-element.47), channel_id=1, source_target_pairs={{0,16},{16,0},{32,48},{48,32},{64,80},{80,64},{96,112},{112,96},{1... | collective-permute-start | bytes 1966088 | tf_op jit(solution)/shard_map/ppermute | solution.py:387
  72.6 4.1 %copy-start.3 = (f32[4,57,8,128]{3,2,1,0:T(8,128)}, f32[4,57,8,128]{3,2,1,0:T(8,128)S(1)}, u32[]{:S(2)}) copy-start(f32[4,57,8,128]{3,2,1,0:T(8,128)S(1)} %collective-permute-done.refs_1_.refs_2_) | copy-start | bytes 2801668
  72.6 19.5 %collective-permute-start.7 = (f32[16,80,128]{2,1,0:T(8,128)}, f32[16,80,128]{2,1,0:T(8,128)}, u32[]{:S(2)}, u32[]{:S(2)}) collective-permute-start(f32[16,80,128]{2,1,0:T(8,128)} %get-tuple-element.48), channel_id=1, source_target_pairs={{0,64},{16,80},{32,96},{48,112},{64,0},{80,16},{96,32},{112,48},{1... | collective-permute-start | bytes 1966088 | tf_op jit(solution)/shard_map/ppermute | solution.py:387
  74.1 2.6 copy-start.4
  74.1 30.3 %collective-permute-start.8 = (f32[16,80,128]{2,1,0:T(8,128)}, f32[16,80,128]{2,1,0:T(8,128)}, u32[]{:S(2)}, u32[]{:S(2)}) collective-permute-start(f32[16,80,128]{2,1,0:T(8,128)} %get-tuple-element.49), channel_id=1, source_target_pairs={{0,80},{16,64},{32,112},{48,96},{64,16},{80,0},{96,48},{112,32},{1... | collective-permute-start | bytes 1966088 | tf_op jit(solution)/shard_map/ppermute | solution.py:387
  75.6 1.2 copy-start.5
  75.6 43.7 %collective-permute-start.9 = (f32[16,80,128]{2,1,0:T(8,128)}, f32[16,80,128]{2,1,0:T(8,128)}, u32[]{:S(2)}, u32[]{:S(2)}) collective-permute-start(f32[16,80,128]{2,1,0:T(8,128)} %get-tuple-element.50), channel_id=1, source_target_pairs={{0,32},{16,48},{32,64},{48,80},{64,96},{80,112},{96,0},{112,16},{1... | collective-permute-start | bytes 1966088 | tf_op jit(solution)/shard_map/ppermute | solution.py:387
  88.4 76.0 %collective-permute-start.3 = (f32[4,57,8,128]{3,2,1,0:T(8,128)}, f32[4,57,8,128]{3,2,1,0:T(8,128)}, u32[]{:S(2)}, u32[]{:S(2)}) collective-permute-start(f32[4,57,8,128]{3,2,1,0:T(8,128)} %get-tuple-element.42), channel_id=1, source_target_pairs={{0,1},{1,2},{2,3},{3,0},{4,5},{5,6},{6,7},{7,4},{8,9},{9,10},{10,1... | collective-permute-start | bytes 2801672 | tf_op jit(solution)/shard_map/ppermute | solution.py:394
  90.0 43.1 %collective-permute-start.13 = (f32[4,56,8,128]{3,2,1,0:T(8,128)}, f32[4,56,8,128]{3,2,1,0:T(8,128)S(1)}, u32[]{:S(2)}, u32[]{:S(2)}) collective-permute-start(f32[4,56,8,128]{3,2,1,0:T(8,128)} %get-tuple-element.55), channel_id=1, source_target_pairs={{0,1},{1,2},{2,3},{3,0},{4,5},{5,6},{6,7},{7,4},{8,9},{9,10},{10,1... | collective-permute-start | bytes 2752520 | tf_op jit(solution)/shard_map/ppermute | solution.py:394
  92.1 61.9 %collective-permute-start.14 = (f32[4,56,8,128]{3,2,1,0:T(8,128)}, f32[4,56,8,128]{3,2,1,0:T(8,128)S(1)}, u32[]{:S(2)}, u32[]{:S(2)}) collective-permute-start(f32[4,56,8,128]{3,2,1,0:T(8,128)} %get-tuple-element.56), channel_id=1, source_target_pairs={{0,2},{1,3},{2,0},{3,1},{4,6},{5,7},{6,4},{7,5},{8,10},{9,11},{10,... | collective-permute-start | bytes 2752520 | tf_op jit(solution)/shard_map/ppermute | solution.py:394
  104.4 49.6 %collective-permute-start.15 = (f32[4,56,8,128]{3,2,1,0:T(8,128)}, f32[4,56,8,128]{3,2,1,0:T(8,128)S(1)}, u32[]{:S(2)}, u32[]{:S(2)}) collective-permute-start(f32[4,56,8,128]{3,2,1,0:T(8,128)} %get-tuple-element.57), channel_id=1, source_target_pairs={{0,3},{1,0},{2,1},{3,2},{4,7},{5,4},{6,5},{7,6},{8,11},{9,8},{10,9... | collective-permute-start | bytes 2752520 | tf_op jit(solution)/shard_map/ppermute | solution.py:394
  125.2 129.4 %all-to-all-start = ((f32[16,4,80,128]{3,2,1,0:T(8,128)}), f32[16,4,80,128]{3,2,1,0:T(8,128)}, u32[]{:S(2)}, u32[]{:S(2)}) async-start(f32[16,4,80,128]{3,2,1,0:T(8,128)} %weigh.1), calls=%async_computation | async-start | bytes 5242880 | tf_op jit(solution)/shard_map/all_to_all | solution.py:421
  133.0 21.0 %copy-start.6 = (f32[4,56,8,128]{3,2,1,0:T(8,128)}, f32[4,56,8,128]{3,2,1,0:T(8,128)S(1)}, u32[]{:S(2)}) copy-start(f32[4,56,8,128]{3,2,1,0:T(8,128)S(1)} %collective-permute-done.13.refs_1_.refs_9_) | copy-start | bytes 2752516
  154.0 0.9 copy-start.7
  154.0 1.2 copy-start.8
  158.2 46.7 %collective-permute-start.16 = (f32[4,56,8,128]{3,2,1,0:T(8,128)}, f32[4,56,8,128]{3,2,1,0:T(8,128)S(1)}, u32[]{:S(2)}, u32[]{:S(2)}) collective-permute-start(f32[4,56,8,128]{3,2,1,0:T(8,128)} %get-tuple-element.58), channel_id=1, source_target_pairs={{0,4},{1,5},{2,6},{3,7},{4,8},{5,9},{6,10},{7,11},{8,12},{9,13},{1... | collective-permute-start | bytes 2752520 | tf_op jit(solution)/shard_map/ppermute | solution.py:394
  159.4 49.9 %collective-permute-start.17 = (f32[4,56,8,128]{3,2,1,0:T(8,128)}, f32[4,56,8,128]{3,2,1,0:T(8,128)S(1)}, u32[]{:S(2)}, u32[]{:S(2)}) collective-permute-start(f32[4,56,8,128]{3,2,1,0:T(8,128)} %get-tuple-element.59), channel_id=1, source_target_pairs={{0,8},{1,9},{2,10},{3,11},{4,12},{5,13},{6,14},{7,15},{8,0},{9,1},... | collective-permute-start | bytes 2752520 | tf_op jit(solution)/shard_map/ppermute | solution.py:394
  159.8 49.8 %collective-permute-start.18 = (f32[4,56,8,128]{3,2,1,0:T(8,128)}, f32[4,56,8,128]{3,2,1,0:T(8,128)S(1)}, u32[]{:S(2)}, u32[]{:S(2)}) collective-permute-start(f32[4,56,8,128]{3,2,1,0:T(8,128)} %get-tuple-element.60), channel_id=1, source_target_pairs={{0,12},{1,13},{2,14},{3,15},{4,0},{5,1},{6,2},{7,3},{8,4},{9,5},{1... | collective-permute-start | bytes 2752520 | tf_op jit(solution)/shard_map/ppermute | solution.py:394
  162.2 42.1 %collective-permute-start.4 = (f32[4,57,8,128]{3,2,1,0:T(8,128)}, f32[4,57,8,128]{3,2,1,0:T(8,128)S(1)}, u32[]{:S(2)}, u32[]{:S(2)}) collective-permute-start(f32[4,57,8,128]{3,2,1,0:T(8,128)} %get-tuple-element.43), channel_id=1, source_target_pairs={{0,2},{1,3},{2,0},{3,1},{4,6},{5,7},{6,4},{7,5},{8,10},{9,11},{10,... | collective-permute-start | bytes 2801672 | tf_op jit(solution)/shard_map/ppermute | solution.py:394
  164.4 39.9 %collective-permute-start.5 = (f32[4,57,8,128]{3,2,1,0:T(8,128)}, f32[4,57,8,128]{3,2,1,0:T(8,128)S(1)}, u32[]{:S(2)}, u32[]{:S(2)}) collective-permute-start(f32[4,57,8,128]{3,2,1,0:T(8,128)} %get-tuple-element.44), channel_id=1, source_target_pairs={{0,3},{1,0},{2,1},{3,2},{4,7},{5,4},{6,5},{7,6},{8,11},{9,8},{10,9... | collective-permute-start | bytes 2801672 | tf_op jit(solution)/shard_map/ppermute | solution.py:394
  204.2 7.0 %copy-start.9 = (f32[4,57,8,128]{3,2,1,0:T(8,128)}, f32[4,57,8,128]{3,2,1,0:T(8,128)S(1)}, u32[]{:S(2)}) copy-start(f32[4,57,8,128]{3,2,1,0:T(8,128)S(1)} %collective-permute-done.4.refs_6_) | copy-start | bytes 2801668
  204.3 7.0 %copy-start.10 = (f32[4,57,8,128]{3,2,1,0:T(8,128)}, f32[4,57,8,128]{3,2,1,0:T(8,128)S(1)}, u32[]{:S(2)}) copy-start(f32[4,57,8,128]{3,2,1,0:T(8,128)S(1)} %collective-permute-done.5.refs_7_) | copy-start | bytes 2801668
  205.0 6.3 %copy-start.11 = (f32[4,56,8,128]{3,2,1,0:T(8,128)}, f32[4,56,8,128]{3,2,1,0:T(8,128)S(1)}, u32[]{:S(2)}) copy-start(f32[4,56,8,128]{3,2,1,0:T(8,128)S(1)} %collective-permute-done.16.refs_12_) | copy-start | bytes 2752516
  209.3 0.9 copy-start.12
  210.3 1.0 copy-start.13
  211.2 43.4 %copy-start.1 = (s32[4,4,2,128]{3,2,1,0:T(2,128)S(1)}, s32[4,4,2,128]{3,2,1,0:T(2,128)}, u32[]{:S(2)}) copy-start(s32[4,4,2,128]{3,2,1,0:T(2,128)} %maximum_convert_fusion) | copy-start | bytes 49156
  211.2 43.4 %copy-start.2 = (f32[32]{0:T(128)S(1)}, f32[32]{0:T(128)}, u32[]{:S(2)}) copy-start(f32[32]{0:T(128)} %reshape.10.refs_0_.refs_1_) | copy-start | bytes 388
  221.6 10.8 %collective-permute-start.19 = (f32[512,128]{1,0:T(8,128)}, f32[512,128]{1,0:T(8,128)S(1)}, u32[]{:S(2)}, u32[]{:S(2)}) collective-permute-start(f32[512,128]{1,0:T(8,128)} %get-tuple-element.62), channel_id=1, source_target_pairs={{0,16},{16,0},{32,48},{48,32},{64,80},{80,64},{96,112},{112,96},{1... | collective-permute-start | bytes 786440 | tf_op jit(solution)/shard_map/ppermute | solution.py:387
  221.6 13.7 %collective-permute-start.20 = (f32[512,128]{1,0:T(8,128)}, f32[512,128]{1,0:T(8,128)S(1)}, u32[]{:S(2)}, u32[]{:S(2)}) collective-permute-start(f32[512,128]{1,0:T(8,128)} %get-tuple-element.63), channel_id=1, source_target_pairs={{0,64},{16,80},{32,96},{48,112},{64,0},{80,16},{96,32},{112,48},{1... | collective-permute-start | bytes 786440 | tf_op jit(solution)/shard_map/ppermute | solution.py:387
  222.5 17.6 %collective-permute-start.21 = (f32[512,128]{1,0:T(8,128)}, f32[512,128]{1,0:T(8,128)S(1)}, u32[]{:S(2)}, u32[]{:S(2)}) collective-permute-start(f32[512,128]{1,0:T(8,128)} %get-tuple-element.64), channel_id=1, source_target_pairs={{0,80},{16,64},{32,112},{48,96},{64,16},{80,0},{96,48},{112,32},{1... | collective-permute-start | bytes 786440 | tf_op jit(solution)/shard_map/ppermute | solution.py:387
  224.9 18.3 %collective-permute-start.22 = (f32[512,128]{1,0:T(8,128)}, f32[512,128]{1,0:T(8,128)S(1)}, u32[]{:S(2)}, u32[]{:S(2)}) collective-permute-start(f32[512,128]{1,0:T(8,128)} %get-tuple-element.65), channel_id=1, source_target_pairs={{0,32},{16,48},{32,64},{48,80},{64,96},{80,112},{96,0},{112,16},{1... | collective-permute-start | bytes 786440 | tf_op jit(solution)/shard_map/ppermute | solution.py:387
  232.3 16.5 %collective-permute-start.23 = (f32[512,128]{1,0:T(8,128)}, f32[512,128]{1,0:T(8,128)S(1)}, u32[]{:S(2)}, u32[]{:S(2)}) collective-permute-start(f32[512,128]{1,0:T(8,128)} %get-tuple-element.66), channel_id=1, source_target_pairs={{0,48},{16,32},{32,80},{48,64},{64,112},{80,96},{96,16},{112,0},{1... | collective-permute-start | bytes 786440 | tf_op jit(solution)/shard_map/ppermute | solution.py:387
  232.3 17.8 %collective-permute-start.24 = (f32[512,128]{1,0:T(8,128)}, f32[512,128]{1,0:T(8,128)S(1)}, u32[]{:S(2)}, u32[]{:S(2)}) collective-permute-start(f32[512,128]{1,0:T(8,128)} %get-tuple-element.67), channel_id=1, source_target_pairs={{0,96},{16,112},{32,0},{48,16},{64,32},{80,48},{96,64},{112,80},{1... | collective-permute-start | bytes 786440 | tf_op jit(solution)/shard_map/ppermute | solution.py:387
  235.3 19.4 %collective-permute-start.25 = (f32[512,128]{1,0:T(8,128)}, f32[512,128]{1,0:T(8,128)S(1)}, u32[]{:S(2)}, u32[]{:S(2)}) collective-permute-start(f32[512,128]{1,0:T(8,128)} %get-tuple-element.68), channel_id=1, source_target_pairs={{0,112},{16,96},{32,16},{48,0},{64,48},{80,32},{96,80},{112,64},{1... | collective-permute-start | bytes 786440 | tf_op jit(solution)/shard_map/ppermute | solution.py:387
  254.6 1.0 copy-start
